TPU v7x, 256 devices: a whole 4x4x8 slice. The times are simulated.
256 devices in a mesh: dp: 32 (over z_hi, y, core), level: 8 (over x, z_lo).
Axes of the slice: x: 4, y: 4, z: 8 (z_hi: 4, z_lo: 2; z = z_hi * 2 + z_lo), core: 2. Of those that a mesh axis runs over, the one named last changes fastest.
Arguments:
- token_ids: int32 [32, 8, 1536], P('dp', 'level'), may hold values from 0 to 1023
- decoded_mask: int32 [32, 8, 1536], P('dp', 'level'), may hold values 0 or 1
- levels_done: int32 [32], P('dp'), may hold values from 0 to 7
- code_tables: bfloat16 [8, 1024, 1024], P('level'), may hold values from -6 to 6
- mask_vectors: bfloat16 [8, 1024], P('level'), may hold values from -6 to 6
- w_qkv: bfloat16 [3, 1024, 1024], P(None, 'dp', 'level'), may hold values from -6 to 6
- w_out: bfloat16 [1024, 1024], P('level', 'dp'), may hold values from -0.1875 to 0.1875
- w_expand: bfloat16 [1024, 2048], P('dp'), may hold values from -0.1875 to 0.1875
- w_depth: bfloat16 [5, 1024], replicated, may hold values from -2.5 to 2.5
- w_project: bfloat16 [1024, 1024], P('dp'), may hold values from -0.1875 to 0.1875
- level_heads: bfloat16 [8, 1024, 1024], P('level'), may hold values from -0.1875 to 0.1875
Outputs:
- logits: bfloat16 [32, 8, 1536, 1024], P('dp', 'level')
Inputs may be any that keep to these rules, and one draw needn't show every extreme that they name: `levels_done`: levels below it are fully decoded; the level equal to it is the one being decoded.
All inputs are finite; a program needn't handle non-finite values. No bound on the sum of `decoded_mask` on one device may be relied on, other than what follows from the above.
Results may differ from a plain program's by a relative error of at most 0.006.
Values may be sent and summed in bfloat16 or wider, within the bound.
A program may use at most 128 MiB of HBM per device.

v0:
```python
import jax
import jax.numpy as jnp
from jax import lax
from jax.sharding import PartitionSpec as P

HEADS = 16


def copy_for_each(x, axis):
    copies = jnp.broadcast_to(x, (lax.axis_size(axis), *x.shape))
    return lax.all_to_all(copies, axis, split_axis=0, concat_axis=0, tiled=True)


def laid_out(tiles, dim):
    tiles = jnp.moveaxis(tiles, 0, dim)
    dims = tiles.shape
    return tiles.reshape(*dims[:dim], dims[dim] * dims[dim + 1], *dims[dim + 2 :])


def gather_directly(x, axis, dim):
    tiles = copy_for_each(x, axis)
    return laid_out(tiles, dim)


def side_by_side(arrays, axis, dim, along):
    ends, at = ([], 0)
    for a in arrays[:-1]:
        at += a.shape[along]
        ends.append(at)
    both = jnp.concatenate(arrays, axis=along)
    return tuple(jnp.split(lax.all_gather(both, axis, axis=dim, tiled=True), ends, axis=along))


def with_halo(x, sides, width):
    for axis, dim in sides:
        devices, length = (lax.axis_size(axis), x.shape[dim])
        up = [(i, (i + 1) % devices) for i in range(devices - 1)]
        down = [(j, i) for i, j in up]
        last = lax.slice_in_dim(x, length - width, length, axis=dim)
        leading = lax.slice_in_dim(x, 0, width, axis=dim)
        before = lax.ppermute(last, axis, up)
        after = lax.ppermute(leading, axis, down)
        x = jnp.concatenate([before, x, after], axis=dim)
    return x


def layer_norm(values):
    centered = values - jnp.mean(values, axis=-1, keepdims=True)
    variance = jnp.mean(centered * centered, axis=-1, keepdims=True)
    return centered * lax.rsqrt(variance + 1e-05)


def contract_with(left, shard_piece):
    return jnp.dot(left, shard_piece, preferred_element_type=jnp.float32)


def contract_three(left, shard_piece):
    return jnp.einsum("fk,jkc->jfc", left, shard_piece, preferred_element_type=jnp.float32)


def body(
    token_ids,
    decoded_mask,
    levels_done,
    code_tables,
    mask_vectors,
    w_qkv,
    w_out,
    w_expand,
    w_depth,
    w_project,
    level_heads,
):
    frames = token_ids.shape[2]
    model_width = code_tables.shape[2]
    groups = lax.axis_size("level")
    level_index = lax.axis_index("level")
    local_rows = frames // groups
    head_dim = model_width // HEADS
    scale = head_dim ** (-0.5)
    id_row = token_ids[0, 0]
    flag_row = decoded_mask[0, 0]
    done_count = levels_done[0]
    own_table = code_tables[0]
    fill_row = mask_vectors[0].astype(jnp.float32)
    all_live = level_index < done_count
    current = level_index == done_count
    use_token = all_live | current & (flag_row == 1)
    codes = lax.broadcasted_iota(jnp.int32, (frames, own_table.shape[0]), 1)
    onehot = (id_row[:, None] == codes).astype(jnp.bfloat16)
    picked = jnp.dot(onehot, own_table, preferred_element_type=jnp.float32)
    level_terms = (
        jnp.where(use_token[:, None], picked, fill_row[None, :])
        .astype(jnp.bfloat16)
        .reshape(groups, local_rows, model_width)
    )
    received = lax.all_to_all(level_terms, "level", split_axis=0, concat_axis=0, tiled=True)
    own_rows = jnp.sum(received, axis=0, dtype=jnp.float32)
    normed = layer_norm(own_rows).astype(jnp.bfloat16)
    full_columns = gather_directly(w_qkv, "level", 2)
    projected = contract_three(
        normed, lax.all_gather(full_columns, "dp", axis=1, tiled=True)
    ).astype(jnp.bfloat16)
    queries = projected[0].reshape(local_rows, HEADS, head_dim)
    running_max = jnp.full((HEADS, local_rows), -1e30, jnp.float32)
    accumulated = jnp.zeros((local_rows, HEADS, head_dim), jnp.float32)
    key_piece, value_piece = side_by_side((projected[1], projected[2]), "level", 0, 1)
    piece_rows = key_piece.shape[0]
    key_three = key_piece.reshape(piece_rows, HEADS, head_dim)
    value_three = value_piece.reshape(piece_rows, HEADS, head_dim)
    scores = (
        jnp.einsum("qhd,khd->hqk", queries, key_three, preferred_element_type=jnp.float32) * scale
    )
    new_max = jnp.maximum(running_max, jnp.max(scores, axis=-1))
    shrink = jnp.exp(running_max - new_max)
    weights = jnp.exp(scores - new_max[:, :, None])
    weight_sum = jnp.sum(weights, axis=-1)
    added = jnp.einsum(
        "hqk,khd->qhd",
        weights.astype(jnp.bfloat16),
        value_three,
        preferred_element_type=jnp.float32,
    )
    accumulated = accumulated * shrink.T[:, :, None] + added
    running_max, weight_sum, accumulated = (new_max, weight_sum, accumulated)
    attended = (
        (accumulated / weight_sum.T[:, :, None])
        .reshape(local_rows, model_width)
        .astype(jnp.bfloat16)
    )
    out_full = gather_directly(w_out, "level", 0)
    after_attn = own_rows + jnp.dot(
        attended,
        lax.all_gather(out_full, "dp", axis=1, tiled=True),
        preferred_element_type=jnp.float32,
    )
    normed_two = layer_norm(after_attn).astype(jnp.bfloat16)
    gate_linear = contract_with(normed_two, lax.all_gather(w_expand, "dp", axis=0, tiled=True))
    gated = (gate_linear[:, :model_width] * jax.nn.sigmoid(gate_linear[:, model_width:])).astype(
        jnp.bfloat16
    )
    half_width = w_depth.shape[0] // 2
    padded = with_halo(gated, (("level", 0),), half_width)
    conv = jnp.zeros((local_rows, model_width), jnp.float32)
    for tap_index in range(w_depth.shape[0]):
        conv = conv + padded[tap_index : tap_index + local_rows].astype(jnp.float32) * w_depth[
            tap_index
        ].astype(jnp.float32)
    activated = (conv * jax.nn.sigmoid(conv)).astype(jnp.bfloat16)
    after_conv = after_attn + contract_with(
        activated, lax.all_gather(w_project, "dp", axis=0, tiled=True)
    )
    final_norm = layer_norm(after_conv).astype(jnp.bfloat16)
    own_head = level_heads[0]
    logits = jnp.dot(
        lax.all_gather(final_norm, "level", axis=0, tiled=True),
        own_head,
        preferred_element_type=jnp.float32,
    ).astype(jnp.bfloat16)
    return logits[None, None]


def solution(mesh):
    return jax.shard_map(
        body,
        mesh=mesh,
        in_specs=(
            P("dp", "level", None),
            P("dp", "level", None),
            P("dp"),
            P("level", None, None),
            P("level", None),
            P(None, "dp", "level"),
            P("level", "dp"),
            P("dp", None),
            P(),
            P("dp", None),
            P("level", None, None),
        ),
        out_specs=P("dp", "level", None, None),
        check_vma=False,
    )
```

profile of v0, /device:TPU:1, one launch (start us, length us, event | category | flops | bytes accessed | tf_op | source)
XLA Modules:
  0.0 501.6 jit_solution(8657905231968769645)
XLA Ops:
  6.5 0.9 broadcast_in_dim.57
  7.5 11.9 %all_to_all.15 = bf16[8,3,32,128]{3,2,1,0:T(8,128)(2,1)S(1)} all-to-all(bf16[8,3,32,128]{3,2,1,0:T(8,128)(2,1)S(1)} %broadcast_in_dim.57), channel_id=1, replica_groups=mesh['dp'=32,'level'=8] {'level'}, dimensions={0} | all-to-all | bytes 393216 | tf_op jit(solution)/shard_map/all_to_all | solution.py:11
  19.4 0.7 copy_bitcast_fusion
  20.1 0.7 broadcast_in_dim.61
  21.5 0.7 reduce.2
  22.2 0.7 or_reduce_fusion
  22.9 4.3 select_convert_fusion
  27.2 60.7 %all_to_all.16 = bf16[8,192,1024]{2,1,0:T(8,128)(2,1)S(1)} all-to-all(bf16[8,192,1024]{2,1,0:T(8,128)(2,1)S(1)} %bitcast.63), channel_id=1, replica_groups=mesh['dp'=32,'level'=8] {'level'}, dimensions={0} | all-to-all | bytes 6291456 | tf_op jit(solution)/shard_map/all_to_all | solution.py:97
  87.9 1.8 convert_reduce_fusion
  90.0 13.5 %all-gather.7.cloned.1.call-done = bf16[3,1024,1024]{2,1,0:T(8,128)(2,1)} async-done(((bf16[3,32,1024]{2,1,0:T(8,128)(2,1)}), bf16[3,1024,1024]{2,1,0:T(8,128)(2,1)}) %all-gather.7.cloned.1.call-update) | async-done | bytes 6291472 | tf_op jit(solution)/shard_map/all_gather | solution.py:102
  103.5 4.2 fusion.11
  107.8 0.9 pad_maximum_fusion
  108.8 9.0 %all_to_all.17 = bf16[8,128,32]{1,2,0:T(8,128)(2,1)S(1)} all-to-all(bf16[8,128,32]{1,2,0:T(8,128)(2,1)S(1)} %broadcast_in_dim.59), channel_id=1, replica_groups=mesh['dp'=32,'level'=8] {'level'}, dimensions={0} | all-to-all | bytes 131072 | tf_op jit(solution)/shard_map/all_to_all | solution.py:11
  117.8 0.6 copy_bitcast_fusion.1
  119.9 119.0 %all-gather.9.cloned.1.call-done = bf16[1536,2048]{1,0:T(8,128)(2,1)} async-done(((bf16[192,2048]{1,0:T(8,128)(2,1)}), bf16[1536,2048]{1,0:T(8,128)(2,1)}) %all-gather.9.cloned.1.call-update) | async-done | bytes 6291472 | tf_op jit(solution)/shard_map/all_gather | solution.py:31
  238.9 6.3 %fusion.45 = (bf16[1536,1024]{1,0:T(8,128)(2,1)}, bf16[1536,1024]{1,0:T(8,128)(2,1)}) fusion(bf16[1536,2048]{1,0:T(8,128)(2,1)} %all-gather.9.cloned.1.call-done), kind=kLoop, calls=%fused_computation.81 | loop fusion | bytes 12582912 | tf_op jit(solution)/shard_map/split | solution.py:31
  245.2 4.7 copy.27
  249.9 4.7 copy.26
  254.6 11.1 %multiply_reduce_fusion = (f32[16,192]{1,0:T(8,128)S(1)}, f32[16,192,1536]{2,1,0:T(8,128)}) fusion(bf16[192,16,64]{0,2,1:T(8,128)(2,1)S(1)} %bitcast.61, bf16[1536,16,64]{0,2,1:T(8,128)(2,1)} %bitcast.60), kind=kOutput, calls=%fused_computation.1 | convolution fusion | flops 613413888 | bytes 22425600 | tf_op jit(solution)/shard_map/qhd,khd->hqk/dot_general | solution.py:112
  265.7 9.6 %fusion = f32[16,192]{1,0:T(8,128)S(1)} fusion(f32[16,192,1536]{2,1,0:T(8,128)} %get-tuple-element.22, f32[16,192]{1,0:T(8,128)S(1)} %get-tuple-element.20), kind=kLoop, calls=%fused_computation.2 | loop fusion | flops 14152704 | bytes 18898944 | tf_op jit(solution)/shard_map/reduce_sum | solution.py:117
  275.3 11.1 %divide_convert_fusion = bf16[192,16,64]{0,2,1:T(8,128)(2,1)S(1)} fusion(bf16[1536,16,64]{0,2,1:T(8,128)(2,1)} %bitcast.62, f32[16,192,1536]{2,1,0:T(8,128)} %get-tuple-element.22, f32[16,192]{1,0:T(8,128)S(1)} %get-tuple-element.20, f32[192,16]{0,1:T(8,128)S(1)} %bitcast.65, f32[192,16]{0,1:T(8,128)S(1)} %get-tuple-element.19), kind=kOutput, calls=%fused_computation.23 | convolution fusion | flops 618725376 | bytes 22450176 | tf_op jit(solution)/shard_map/hqk,khd->qhd/dot_general | solution.py:118
  286.4 11.3 %all-gather.11.cloned.1.call-done = bf16[1024,1024]{0,1:T(8,128)(2,1)} async-done(((bf16[1024,32]{0,1:T(8,128)(2,1)}), bf16[1024,1024]{0,1:T(8,128)(2,1)}) %all-gather.11.cloned.1.call-update) | async-done | bytes 2097168 | tf_op jit(solution)/shard_map/all_gather | solution.py:134
  297.7 2.5 fusion.48
  300.5 57.0 %all-gather.13.cloned.1.call-done = bf16[1024,2048]{1,0:T(8,128)(2,1)} async-done(((bf16[32,2048]{1,0:T(8,128)(2,1)}), bf16[1024,2048]{1,0:T(8,128)(2,1)}) %all-gather.13.cloned.1.call-update) | async-done | bytes 4194320 | tf_op jit(solution)/shard_map/all_gather | solution.py:138
  357.5 3.2 fusion.29
  360.9 1.3 collective-permute-start.1
  362.2 4.2 collective-permute-start
  366.5 46.3 %all-gather.15.cloned.1.call-done = bf16[1024,1024]{1,0:T(8,128)(2,1)} async-done(((bf16[32,1024]{1,0:T(8,128)(2,1)}), bf16[1024,1024]{1,0:T(8,128)(2,1)}) %all-gather.15.cloned.1.call-update) | async-done | bytes 2097168 | tf_op jit(solution)/shard_map/all_gather | solution.py:151
  412.8 2.7 fusion.49
  415.7 0.9 multiply_convert_fusion
  416.7 70.3 %all-gather.17.cloned.1.call-done = bf16[1536,1024]{1,0:T(8,128)(2,1)} async-done(((bf16[192,1024]{1,0:T(8,128)(2,1)}), bf16[1536,1024]{1,0:T(8,128)(2,1)}) %all-gather.17.cloned.1.call-update) | async-done | bytes 3145744 | tf_op jit(solution)/shard_map/all_gather | solution.py:156
  487.0 7.8 %fusion.7 = bf16[1,1,1536,1024]{3,2,1,0:T(8,128)(2,1)} fusion(bf16[1536,1024]{1,0:T(8,128)(2,1)} %all-gather.17.cloned.1.call-done, bf16[1,1024,1024]{2,1,0:T(8,128)(2,1)} %param.21), kind=kOutput, calls=%fused_computation.13 | convolution fusion | flops 3222798336 | bytes 8388608 | tf_op jit(solution)/shard_map/dot_general | solution.py:155
  (38 shorter events, 2.6 us)
Async XLA Ops:
  6.5 16.4 %copy-start = (bf16[1,1024,1024]{2,1,0:T(8,128)(2,1)S(1)}, bf16[1,1024,1024]{2,1,0:T(8,128)(2,1)}, u32[]{:S(2)}) copy-start(bf16[1,1024,1024]{2,1,0:T(8,128)(2,1)} %param.14) | copy-start | bytes 6291460
  6.5 96.9 %all-gather.7.cloned.1.call-start = ((), (), s32[]{:S(2)}) async-start(), calls=%async_computation.3 | async-start | bytes 6488064 | tf_op jit(solution)/shard_map/all_gather | solution.py:102
  20.1 218.8 %all-gather.9.cloned.1.call-start = ((), (), s32[]{:S(2)}) async-start(), calls=%async_computation.4 | async-start | bytes 7077888 | tf_op jit(solution)/shard_map/all_gather | solution.py:31
  107.7 1.1 copy-start.3
  108.8 189.0 %all-gather.11.cloned.1.call-start = ((), (), s32[]{:S(2)}) async-start(), calls=%async_computation.5 | async-start | bytes 2162688 | tf_op jit(solution)/shard_map/all_gather | solution.py:134
  118.5 239.0 %all-gather.13.cloned.1.call-start = ((), (), s32[]{:S(2)}) async-start(), calls=%async_computation.6 | async-start | bytes 4325376 | tf_op jit(solution)/shard_map/all_gather | solution.py:138
  119.1 293.7 %all-gather.15.cloned.1.call-start = ((), (), s32[]{:S(2)}) async-start(), calls=%async_computation.7 | async-start | bytes 2162688 | tf_op jit(solution)/shard_map/all_gather | solution.py:151
  119.6 367.3 %all-gather.17.cloned.1.call-start = ((), (), s32[]{:S(2)}) async-start(), calls=%async_computation.8 | async-start | bytes 3538944 | tf_op jit(solution)/shard_map/all_gather | solution.py:156
  300.5 66.0 %copy-start.2 = (bf16[5,1024]{1,0:T(8,128)(2,1)S(1)}, bf16[5,1024]{1,0:T(8,128)(2,1)}, u32[]{:S(2)}) copy-start(bf16[5,1024]{1,0:T(8,128)(2,1)} %param.19) | copy-start | bytes 30724
  360.9 51.8 %collective-permute-start.1 = (bf16[2,1024]{1,0:T(2,128)(2,1)S(1)}, bf16[2,1024]{1,0:T(2,128)(2,1)S(1)}, u32[]{:S(2)}, u32[]{:S(2)}) collective-permute-start(bf16[2,1024]{1,0:T(2,128)(2,1)S(1)} %get-tuple-element.13), channel_id=1, source_target_pairs={{1,0},{2,1},{3,2},{4,3},{5,4},{6,5},{7,6},{9,8},{10,9},{11,10},{12... | collective-permute-start | bytes 12296 | tf_op jit(solution)/shard_map/ppermute | solution.py:42
  362.2 50.5 %collective-permute-start = (bf16[2,1024]{1,0:T(2,128)(2,1)S(1)}, bf16[2,1024]{1,0:T(2,128)(2,1)S(1)}, u32[]{:S(2)}, u32[]{:S(2)}) collective-permute-start(bf16[2,1024]{1,0:T(2,128)(2,1)S(1)} %get-tuple-element.12), channel_id=1, source_target_pairs={{0,1},{1,2},{2,3},{3,4},{4,5},{5,6},{6,7},{8,9},{9,10},{10,11},{11... | collective-permute-start | bytes 12296 | tf_op jit(solution)/shard_map/ppermute | solution.py:41
  487.0 7.8 %copy-start.1 = (bf16[1,1024,1024]{2,1,0:T(8,128)(2,1)S(1)}, bf16[1,1024,1024]{2,1,0:T(8,128)(2,1)}, u32[]{:S(2)}) copy-start(bf16[1,1024,1024]{2,1,0:T(8,128)(2,1)} %param.14) | copy-start | bytes 6291460
Sparse Core Ops, SparseCore 0:
  20.2 83.2 all-gather.6
  108.9 129.9 all-gather.8
  241.5 56.1 all-gather.10
  300.1 57.3 all-gather.12
  359.9 52.8 all-gather.14
  416.8 70.1 all-gather.16
where the time goes:
time: 502 us
  waiting for transfers between devices  318 us (63%)
  blocking collectives  81.6 us (16%)
  matrix products  46.9 us (9%)
  local copies, waits for them, and re-layouts  18.2 us (4%)
  other arithmetic  16.4 us (3%)
  between operations  14.3 us (3%)
  starting transfers between devices  5.7 us (1%)
    all_gather x1, waiting for transfers between devices, side_by_side(): lax.all_gather(both, axis, axis=dim, tiled=True)  119 us
    all_gather x1, waiting for transfers between devices, body(): lax.all_gather(final_norm, 'level', axis=0, tiled=True)  70.3 us
    all_to_all x1, blocking collectives, body(): lax.all_to_all(level_terms, 'level', split_axis=0, concat_axis=0, tiled=T...  60.7 us
    all_gather x1, waiting for transfers between devices, body(): lax.all_gather(w_expand, 'dp', axis=0, tiled=True)  57 us
    all_gather x1, waiting for transfers between devices, body(): lax.all_gather(w_project, 'dp', axis=0, tiled=True)  46.3 us
    all_to_all x2, blocking collectives, copy_for_each(): return lax.all_to_all(copies, axis, split_axis=0, concat_axis=0, tiled=True)  20.9 us
    split x3, local copies, waits for them, and re-layouts, side_by_side(): jnp.split(lax.all_gather(both, axis, axis=dim, tiled=True), ends, axis=al...  15.7 us
    all_gather x1, waiting for transfers between devices, body(): lax.all_gather(full_columns, 'dp', axis=1, tiled=True)  13.5 us
  transfers between devices with their start and end apart: 8, of which 6 were waited for; matrix products, arithmetic and copies ran while one was open for 13% of the time, Pallas kernels for 0%

commit v1 on v0

--- a/solution.py
+++ b/solution.py
@@ -147,9 +147,14 @@
             tap_index
         ].astype(jnp.float32)
     activated = (conv * jax.nn.sigmoid(conv)).astype(jnp.bfloat16)
-    after_conv = after_attn + contract_with(
-        activated, lax.all_gather(w_project, "dp", axis=0, tiled=True)
-    )
+
+    def cards_manage(dev_axis, sample):
+        y1 = tuple((sample for _ in range(jax.lax.psum(1, dev_axis))))
+        r2 = jnp.stack(y1)
+        base_arr = jax.lax.all_to_all(r2, dev_axis, 0, 0)
+        return jnp.concatenate(base_arr, axis=0)
+
+    after_conv = after_attn + contract_with(activated, cards_manage("dp", w_project))
     final_norm = layer_norm(after_conv).astype(jnp.bfloat16)
     own_head = level_heads[0]
     logits = jnp.dot(

time: 502 us -> 505 us (level)
  starting transfers between devices: 5.7 us -> 14.8 us
  waiting for transfers between devices: 318 us -> 311 us
    all_gather x1 -> x0, waiting for transfers between devices: 46.3 us -> none  [body(): lax.all_gather(w_project, 'dp', axis=0, tiled=True)]
    all_gather x1, waiting for transfers between devices: 119 us -> 154 us  [side_by_side(): lax.all_gather(both, axis, axis=dim, tiled=True)]
    all_to_all x0 -> x1, starting transfers between devices: none -> 9.16 us  [cards_manage(): base_arr = jax.lax.all_to_all(r2, dev_axis, 0, 0)]
where the time goes in v1:
time: 505 us; the launch traced here: 504 us
  waiting for transfers between devices  311 us (62%)
  blocking collectives  81.6 us (16%)
  matrix products  46.9 us (9%)
  local copies, waits for them, and re-layouts  19.8 us (4%)
  other arithmetic  16.4 us (3%)
  starting transfers between devices  14.8 us (3%)
  between operations  14 us (3%)
    all_gather x1, waiting for transfers between devices, side_by_side(): lax.all_gather(both, axis, axis=dim, tiled=True)  154 us
    all_gather x1, waiting for transfers between devices, body(): lax.all_gather(final_norm, 'level', axis=0, tiled=True)  73.9 us
    all_to_all x1, blocking collectives, body(): lax.all_to_all(level_terms, 'level', split_axis=0, concat_axis=0, tiled=T...  60.7 us
    all_gather x1, waiting for transfers between devices, body(): lax.all_gather(w_expand, 'dp', axis=0, tiled=True)  57 us
    all_to_all x2, blocking collectives, copy_for_each(): return lax.all_to_all(copies, axis, split_axis=0, concat_axis=0, tiled=True)  20.9 us
    split x3, local copies, waits for them, and re-layouts, side_by_side(): jnp.split(lax.all_gather(both, axis, axis=dim, tiled=True), ends, axis=al...  15.7 us
    all_gather x1, waiting for transfers between devices, body(): lax.all_gather(full_columns, 'dp', axis=1, tiled=True)  13.5 us
    all_gather x1, waiting for transfers between devices, body(): lax.all_gather(out_full, 'dp', axis=1, tiled=True)  11.4 us
  transfers between devices with their start and end apart: 8, of which 6 were waited for; matrix products, arithmetic and copies ran while one was open for 13% of the time, Pallas kernels for 0%

profile of v1, /device:TPU:1, one launch (start us, length us, event | category | flops | bytes accessed | tf_op | source)
XLA Modules:
  0.0 504.1 jit_solution(9351163729252406555)
XLA Ops:
  6.5 0.9 broadcast_in_dim.57
  7.5 11.9 %all_to_all.20 = bf16[8,3,32,128]{3,2,1,0:T(8,128)(2,1)S(1)} all-to-all(bf16[8,3,32,128]{3,2,1,0:T(8,128)(2,1)S(1)} %broadcast_in_dim.57), channel_id=1, replica_groups=mesh['dp'=32,'level'=8] {'level'}, dimensions={0} | all-to-all | bytes 393216 | tf_op jit(solution)/shard_map/all_to_all | solution.py:11
  19.4 0.7 copy_bitcast_fusion
  20.1 0.7 broadcast_in_dim.61
  21.5 0.7 reduce.2
  22.2 0.7 or_reduce_fusion
  22.9 4.3 select_convert_fusion
  27.2 60.7 %all_to_all.21 = bf16[8,192,1024]{2,1,0:T(8,128)(2,1)S(1)} all-to-all(bf16[8,192,1024]{2,1,0:T(8,128)(2,1)S(1)} %bitcast.64), channel_id=1, replica_groups=mesh['dp'=32,'level'=8] {'level'}, dimensions={0} | all-to-all | bytes 6291456 | tf_op jit(solution)/shard_map/all_to_all | solution.py:97
  87.9 1.8 convert_reduce_fusion
  90.0 13.5 %all-gather.6.cloned.1.call-done = bf16[3,1024,1024]{2,1,0:T(8,128)(2,1)} async-done(((bf16[3,32,1024]{2,1,0:T(8,128)(2,1)}), bf16[3,1024,1024]{2,1,0:T(8,128)(2,1)}) %all-gather.6.cloned.1.call-update) | async-done | bytes 6291472 | tf_op jit(solution)/shard_map/all_gather | solution.py:102
  103.5 4.2 fusion.11
  107.8 0.9 pad_maximum_fusion
  108.9 9.0 %all_to_all.22 = bf16[8,128,32]{1,2,0:T(8,128)(2,1)S(1)} all-to-all(bf16[8,128,32]{1,2,0:T(8,128)(2,1)S(1)} %broadcast_in_dim.59), channel_id=1, replica_groups=mesh['dp'=32,'level'=8] {'level'}, dimensions={0} | all-to-all | bytes 131072 | tf_op jit(solution)/shard_map/all_to_all | solution.py:11
  119.1 1.6 stack.2
  120.6 9.2 %all-to-all-start.3 = ((bf16[32,32,1024]{2,1,0:T(8,128)(2,1)}), bf16[32,32,1024]{2,1,0:T(8,128)(2,1)}, u32[]{:S(2)}, u32[]{:S(2)}) async-start(bf16[32,32,1024]{2,1,0:T(8,128)(2,1)} %stack.2), calls=%async_computation.3 | async-start | bytes 4194304 | tf_op jit(solution)/shard_map/all_to_all | solution.py:154
  130.1 153.8 %all-gather.8.cloned.1.call-done = bf16[1536,2048]{1,0:T(8,128)(2,1)} async-done(((bf16[192,2048]{1,0:T(8,128)(2,1)}), bf16[1536,2048]{1,0:T(8,128)(2,1)}) %all-gather.8.cloned.1.call-update) | async-done | bytes 6291472 | tf_op jit(solution)/shard_map/all_gather | solution.py:31
  283.9 6.3 %fusion.45 = (bf16[1536,1024]{1,0:T(8,128)(2,1)}, bf16[1536,1024]{1,0:T(8,128)(2,1)}) fusion(bf16[1536,2048]{1,0:T(8,128)(2,1)} %all-gather.8.cloned.1.call-done), kind=kLoop, calls=%fused_computation.81 | loop fusion | bytes 12582912 | tf_op jit(solution)/shard_map/split | solution.py:31
  290.2 4.7 copy.27
  294.9 4.7 copy.26
  299.6 11.1 %multiply_reduce_fusion = (f32[16,192]{1,0:T(8,128)S(1)}, f32[16,192,1536]{2,1,0:T(8,128)}) fusion(bf16[192,16,64]{0,2,1:T(8,128)(2,1)S(1)} %bitcast.62, bf16[1536,16,64]{0,2,1:T(8,128)(2,1)} %bitcast.61), kind=kOutput, calls=%fused_computation.1 | convolution fusion | flops 613413888 | bytes 22425600 | tf_op jit(solution)/shard_map/qhd,khd->hqk/dot_general | solution.py:112
  310.6 9.6 %fusion = f32[16,192]{1,0:T(8,128)S(1)} fusion(f32[16,192,1536]{2,1,0:T(8,128)} %get-tuple-element.22, f32[16,192]{1,0:T(8,128)S(1)} %get-tuple-element.20), kind=kLoop, calls=%fused_computation.2 | loop fusion | flops 14152704 | bytes 18898944 | tf_op jit(solution)/shard_map/reduce_sum | solution.py:117
  320.2 11.1 %divide_convert_fusion = bf16[192,16,64]{0,2,1:T(8,128)(2,1)S(1)} fusion(bf16[1536,16,64]{0,2,1:T(8,128)(2,1)} %bitcast.63, f32[16,192,1536]{2,1,0:T(8,128)} %get-tuple-element.22, f32[16,192]{1,0:T(8,128)S(1)} %get-tuple-element.20, f32[192,16]{0,1:T(8,128)S(1)} %bitcast.66, f32[192,16]{0,1:T(8,128)S(1)} %get-tuple-element.19), kind=kOutput, calls=%fused_computation.23 | convolution fusion | flops 618725376 | bytes 22450176 | tf_op jit(solution)/shard_map/hqk,khd->qhd/dot_general | solution.py:118
  331.3 11.4 %all-gather.10.cloned.1.call-done = bf16[1024,1024]{0,1:T(8,128)(2,1)} async-done(((bf16[1024,32]{0,1:T(8,128)(2,1)}), bf16[1024,1024]{0,1:T(8,128)(2,1)}) %all-gather.10.cloned.1.call-update) | async-done | bytes 2097168 | tf_op jit(solution)/shard_map/all_gather | solution.py:134
  342.7 2.5 fusion.48
  345.5 57.0 %all-gather.12.cloned.1.call-done = bf16[1024,2048]{1,0:T(8,128)(2,1)} async-done(((bf16[32,2048]{1,0:T(8,128)(2,1)}), bf16[1024,2048]{1,0:T(8,128)(2,1)}) %all-gather.12.cloned.1.call-update) | async-done | bytes 4194320 | tf_op jit(solution)/shard_map/all_gather | solution.py:138
  402.4 3.2 fusion.29
  405.9 1.3 collective-permute-start.1
  407.2 4.2 collective-permute-start
  411.9 2.7 fusion.49
  414.9 0.9 multiply_convert_fusion
  415.8 73.9 %all-gather.14.cloned.1.call-done = bf16[1536,1024]{1,0:T(8,128)(2,1)} async-done(((bf16[192,1024]{1,0:T(8,128)(2,1)}), bf16[1536,1024]{1,0:T(8,128)(2,1)}) %all-gather.14.cloned.1.call-update) | async-done | bytes 3145744 | tf_op jit(solution)/shard_map/all_gather | solution.py:161
  489.8 7.8 %fusion.7 = bf16[1,1,1536,1024]{3,2,1,0:T(8,128)(2,1)} fusion(bf16[1536,1024]{1,0:T(8,128)(2,1)} %all-gather.14.cloned.1.call-done, bf16[1,1024,1024]{2,1,0:T(8,128)(2,1)} %param.21), kind=kOutput, calls=%fused_computation.13 | convolution fusion | flops 3222798336 | bytes 8388608 | tf_op jit(solution)/shard_map/dot_general | solution.py:160
  (40 shorter events, 3.2 us)
Async XLA Ops:
  6.5 16.4 %copy-start = (bf16[1,1024,1024]{2,1,0:T(8,128)(2,1)S(1)}, bf16[1,1024,1024]{2,1,0:T(8,128)(2,1)}, u32[]{:S(2)}) copy-start(bf16[1,1024,1024]{2,1,0:T(8,128)(2,1)} %param.14) | copy-start | bytes 6291460
  6.5 96.9 %all-gather.6.cloned.1.call-start = ((), (), s32[]{:S(2)}) async-start(), calls=%async_computation.4 | async-start | bytes 6488064 | tf_op jit(solution)/shard_map/all_gather | solution.py:102
  20.1 263.8 %all-gather.8.cloned.1.call-start = ((), (), s32[]{:S(2)}) async-start(), calls=%async_computation.5 | async-start | bytes 7077888 | tf_op jit(solution)/shard_map/all_gather | solution.py:31
  107.7 1.1 copy-start.4
  107.7 11.4 %copy-start.2 = (bf16[32,1024]{1,0:T(8,128)(2,1)S(1)}, bf16[32,1024]{1,0:T(8,128)(2,1)}, u32[]{:S(2)}) copy-start(bf16[32,1024]{1,0:T(8,128)(2,1)} %param.20) | copy-start | bytes 196612
  108.8 233.9 %all-gather.10.cloned.1.call-start = ((), (), s32[]{:S(2)}) async-start(), calls=%async_computation.6 | async-start | bytes 2162688 | tf_op jit(solution)/shard_map/all_gather | solution.py:134
  118.5 283.9 %all-gather.12.cloned.1.call-start = ((), (), s32[]{:S(2)}) async-start(), calls=%async_computation.7 | async-start | bytes 4325376 | tf_op jit(solution)/shard_map/all_gather | solution.py:138
  120.6 290.8 %all-to-all-start.3 = ((bf16[32,32,1024]{2,1,0:T(8,128)(2,1)}), bf16[32,32,1024]{2,1,0:T(8,128)(2,1)}, u32[]{:S(2)}, u32[]{:S(2)}) async-start(bf16[32,32,1024]{2,1,0:T(8,128)(2,1)} %stack.2), calls=%async_computation.3 | async-start | bytes 4194304 | tf_op jit(solution)/shard_map/all_to_all | solution.py:154
  129.8 360.0 %all-gather.14.cloned.1.call-start = ((), (), s32[]{:S(2)}) async-start(), calls=%async_computation.8 | async-start | bytes 3538944 | tf_op jit(solution)/shard_map/all_gather | solution.py:161
  345.5 66.0 %copy-start.3 = (bf16[5,1024]{1,0:T(8,128)(2,1)S(1)}, bf16[5,1024]{1,0:T(8,128)(2,1)}, u32[]{:S(2)}) copy-start(bf16[5,1024]{1,0:T(8,128)(2,1)} %param.19) | copy-start | bytes 30724
  405.9 5.6 %collective-permute-start.1 = (bf16[2,1024]{1,0:T(2,128)(2,1)S(1)}, bf16[2,1024]{1,0:T(2,128)(2,1)S(1)}, u32[]{:S(2)}, u32[]{:S(2)}) collective-permute-start(bf16[2,1024]{1,0:T(2,128)(2,1)S(1)} %get-tuple-element.13), channel_id=1, source_target_pairs={{1,0},{2,1},{3,2},{4,3},{5,4},{6,5},{7,6},{9,8},{10,9},{11,10},{12... | collective-permute-start | bytes 12296 | tf_op jit(solution)/shard_map/ppermute | solution.py:42
  407.2 4.7 collective-permute-start
  489.8 7.8 %copy-start.1 = (bf16[1,1024,1024]{2,1,0:T(8,128)(2,1)S(1)}, bf16[1,1024,1024]{2,1,0:T(8,128)(2,1)}, u32[]{:S(2)}) copy-start(bf16[1,1024,1024]{2,1,0:T(8,128)(2,1)} %param.14) | copy-start | bytes 6291460
Sparse Core Ops, SparseCore 0:
  20.2 83.2 all-gather.5
  108.9 174.9 all-gather.7
  286.4 56.2 all-gather.9
  345.1 57.2 all-gather.11
  416.0 73.7 all-gather.13
